TPU v7x, 32 devices: a whole 2x2x4 slice. The times are simulated.
32 devices in a mesh: batch: 2 (over x), col: 4 (over z), row: 4 (over y, core).
Axes of the slice: x: 2, y: 2, z: 4, core: 2. Of those that a mesh axis runs over, the one named last changes fastest.
Arguments:
- z_one: bfloat16 [2048, 1024, 64], P(('batch', 'row'), 'col'), parts along dimension 0
- z_two: bfloat16 [2048, 1024, 64], P(('batch', 'row'), 'col'), parts along dimension 0
- mask_one: int32 [2048, 1024], P(('batch', 'row'), 'col'), parts along dimension 0
- mask_two: int32 [2048, 1024], P(('batch', 'row'), 'col'), parts along dimension 0
- ln_in_scale: bfloat16 [64], replicated
- w_a: bfloat16 [64, 64], replicated
- w_a_gate: bfloat16 [64, 64], replicated
- w_b: bfloat16 [64, 64], replicated
- w_b_gate: bfloat16 [64, 64], replicated
- w_gate: bfloat16 [64, 64], replicated
- w_out: bfloat16 [64, 64], replicated
- ln_out_scale: bfloat16 [64], replicated
Outputs:
- output 1: bfloat16 [2048, 1024, 64], P(('batch', 'row'), 'col'), parts along dimension 0
- output 2: bfloat16 [2048, 1024, 64], P(('batch', 'row'), 'col'), parts along dimension 0
There are 2 independent parts. A program takes and returns all parts, laid end to end along the dimension named above; an argument that names none is the same for every part.
All inputs are finite; a program needn't handle non-finite values.
Results may differ from a plain program's by a relative error of at most 0.001.
Values are sent between devices in bfloat16 or wider.
A program may use at most 1 GiB of HBM per device.

v0:
```python
import math
import jax
import jax.numpy as jnp
from jax import lax
from jax.sharding import PartitionSpec as P


def layer_norm(values, scale):
    row_mean = jnp.mean(values, axis=-1, keepdims=True)
    centered = values - row_mean
    variance = jnp.mean(centered * centered, axis=-1, keepdims=True)
    return centered * lax.rsqrt(variance + 1e-5) * scale.astype(jnp.float32)


def tile_update(pair_tile, mask_tile, ln_in_scale, weights, transpose_perm, col_count, ratio):
    w_a, w_a_gate, w_b, w_b_gate, w_gate, w_out, ln_out_scale = weights
    rows_loc, cols_loc, pair_ch = pair_tile.shape
    hidden = w_out.shape[0]
    normed = layer_norm(pair_tile.astype(jnp.float32), ln_in_scale).astype(jnp.bfloat16)

    def project(source, weight):
        return jnp.einsum('ijd,de->ije', source, weight, preferred_element_type=jnp.float32)

    mask_val = mask_tile.astype(jnp.float32)[:, :, None]
    left = (mask_val * jax.nn.sigmoid(project(normed, w_a_gate)) * project(normed, w_a)).astype(jnp.bfloat16)
    right = (mask_val * jax.nn.sigmoid(project(normed, w_b_gate)) * project(normed, w_b)).astype(jnp.bfloat16)
    left_rows = lax.all_gather(left, 'col', axis=1)
    right_moved = lax.ppermute(right, ('col', 'row'), transpose_perm)
    right_rows = lax.all_gather(right_moved, 'row', axis=0).reshape(col_count, ratio, rows_loc, cols_loc, hidden)
    block_rows = math.gcd(rows_loc, 32)
    block_count = rows_loc // block_rows

    def finish(block):
        left_blk, pair_blk, normed_blk = block
        contracted = jnp.einsum('itkc,tujkc->iujc', left_blk, right_rows, preferred_element_type=jnp.float32)
        contracted = contracted.reshape(block_rows, cols_loc, hidden)
        normed_out = layer_norm(contracted, ln_out_scale).astype(jnp.bfloat16)
        update = jnp.einsum('ijc,cd->ijd', normed_out, w_out, preferred_element_type=jnp.float32)
        gate = jax.nn.sigmoid(project(normed_blk, w_gate))
        return (pair_blk.astype(jnp.float32) + gate * update).astype(jnp.bfloat16)

    out_blocks = lax.map(finish, (
        left_rows.reshape(block_count, block_rows, col_count, cols_loc, hidden),
        pair_tile.reshape(block_count, block_rows, cols_loc, pair_ch),
        normed.reshape(block_count, block_rows, cols_loc, pair_ch),
    ))
    return out_blocks.reshape(rows_loc, cols_loc, pair_ch)


def solution(mesh):
    row_count = mesh.shape['row']
    col_count = mesh.shape['col']
    ratio = row_count // col_count
    transpose_perm = [
        (src_col * row_count + src_row, (src_row // ratio) * row_count + src_col * ratio + src_row % ratio)
        for src_row in range(row_count) for src_col in range(col_count)
    ]
    pair_spec = P(('batch', 'row'), 'col', None)
    mask_spec = P(('batch', 'row'), 'col')
    replicated = P()

    def device_fn(z_one, z_two, mask_one, mask_two, ln_in_scale, w_a, w_a_gate, w_b, w_b_gate, w_gate, w_out, ln_out_scale):
        weights = (w_a, w_a_gate, w_b, w_b_gate, w_gate, w_out, ln_out_scale)
        out_one = tile_update(z_one, mask_one, ln_in_scale, weights, transpose_perm, col_count, ratio)
        out_two = tile_update(z_two, mask_two, ln_in_scale, weights, transpose_perm, col_count, ratio)
        return out_one, out_two

    return jax.shard_map(
        device_fn,
        mesh=mesh,
        in_specs=(pair_spec, pair_spec, mask_spec, mask_spec, replicated, replicated, replicated, replicated, replicated, replicated, replicated, replicated),
        out_specs=(pair_spec, pair_spec),
        check_vma=False,
    )
```

profile of v0, /device:TPU:24, one launch (start us, length us, event | category | flops | bytes accessed | tf_op | source)
XLA Modules:
  0.0 2604.0 jit_solution(14808185272356895525)
XLA Ops:
  26.6 13.1 fusion.30
  48.2 11.6 multiply_convert_fusion.3
  60.7 11.5 fusion.44
  72.2 13.3 multiply_convert_fusion.5
  111.6 365.3 %collective-permute-done.1 = bf16[256,256,64]{1,2,0:T(8,128)(2,1)} collective-permute-done((bf16[256,256,64]{1,2,0:T(8,128)(2,1)S(1)}, bf16[256,256,64]{1,2,0:T(8,128)(2,1)}, u32[]{:S(2)}, u32[]{:S(2)}) %collective-permute-start.1) | collective-permute-done | bytes 8388640 | tf_op jit(solution)/shard_map/ppermute | solution.py:28
  477.0 11.5 fusion.38
  502.5 275.2 %collective-permute-done = bf16[256,256,64]{1,2,0:T(8,128)(2,1)} collective-permute-done((bf16[256,256,64]{1,2,0:T(8,128)(2,1)S(1)}, bf16[256,256,64]{1,2,0:T(8,128)(2,1)}, u32[]{:S(2)}, u32[]{:S(2)}) %collective-permute-start) | collective-permute-done | bytes 8388640 | tf_op jit(solution)/shard_map/ppermute | solution.py:28
  777.9 172.7 %all-gather.13.cloned.1.call-done = bf16[256,1024,64]{1,2,0:T(8,128)(2,1)} async-done(((bf16[256,256,64]{1,2,0:T(8,128)(2,1)}), bf16[256,1024,64]{1,2,0:T(8,128)(2,1)}) %all-gather.13.cloned.1.call-update) | async-done | bytes 33554448 | tf_op jit(solution)/shard_map/all_gather | solution.py:27
  950.6 54.7 %reshape.116 = bf16[8,32,4,256,64]{3,2,4,1,0:T(4,128)(2,1)} reshape(bf16[256,1024,64]{1,2,0:T(8,128)(2,1)} %all-gather.13.cloned.1.call-done) | data formatting | bytes 67108864 | tf_op jit(solution)/shard_map/reshape | solution.py:43
  1005.4 871.8 %all-gather.9.cloned.1.call-done = bf16[256,1024,64]{1,2,0:T(8,128)(2,1)} async-done(((bf16[256,256,64]{1,2,0:T(8,128)(2,1)}), bf16[256,1024,64]{1,2,0:T(8,128)(2,1)}) %all-gather.9.cloned.1.call-update) | async-done | bytes 33554448 | tf_op jit(solution)/shard_map/all_gather | solution.py:27
  1877.1 54.7 %reshape.111 = bf16[8,32,4,256,64]{3,2,4,1,0:T(4,128)(2,1)} reshape(bf16[256,1024,64]{1,2,0:T(8,128)(2,1)} %all-gather.9.cloned.1.call-done) | data formatting | bytes 67108864 | tf_op jit(solution)/shard_map/reshape | solution.py:43
  1931.8 152.3 %all-gather.15.cloned.1.call-done = bf16[1024,256,64]{1,2,0:T(8,128)(2,1)} async-done(((bf16[256,256,64]{1,2,0:T(8,128)(2,1)}), bf16[1024,256,64]{1,2,0:T(8,128)(2,1)}) %all-gather.15.cloned.1.call-update) | async-done | bytes 33554448 | tf_op jit(solution)/shard_map/all_gather | solution.py:29
  2084.1 23.3 copy.48
  2111.9 227.8 %while.21 = (s32[]{:T(128)}, bf16[8,32,256,64]{2,3,1,0:T(8,128)(2,1)}, bf16[8,32,256,64]{2,3,1,0:T(8,128)(2,1)}, bf16[8,32,256,64]{2,3,1,0:T(8,128)(2,1)}, bf16[...) while((s32[]{:T(128)}, ...), condition=%wide.region_11.12_spmd, body=%wide.region_8.11_spmd.sunk | while | flops 1215832064 | bytes 62179048 | solution.py:42
  2118.6 16.1 bitcast_reduce_fusion.5
  2147.0 16.1 bitcast_reduce_fusion.5
  2175.5 16.1 bitcast_reduce_fusion.5
  2204.0 16.1 bitcast_reduce_fusion.5
  2232.5 16.1 bitcast_reduce_fusion.5
  2260.9 16.1 bitcast_reduce_fusion.5
  2289.4 16.1 bitcast_reduce_fusion.5
  2317.9 16.1 bitcast_reduce_fusion.5
  2339.7 23.3 copy.40
  2367.5 228.8 %while.20 = (s32[]{:T(128)}, bf16[8,32,256,64]{2,3,1,0:T(8,128)(2,1)}, bf16[8,32,256,64]{2,3,1,0:T(8,128)(2,1)}, bf16[8,32,256,64]{2,3,1,0:T(8,128)(2,1)}, bf16[...) while((s32[]{:T(128)}, ...), condition=%wide.region_5.6_spmd, body=%wide.region_2.5_spmd.sunk | while | flops 1215832064 | bytes 62179048 | solution.py:42
  2374.5 16.1 bitcast_reduce_fusion.4
  2403.1 16.1 bitcast_reduce_fusion.4
  2431.6 16.1 bitcast_reduce_fusion.4
  2460.2 16.1 bitcast_reduce_fusion.4
  2488.8 16.1 bitcast_reduce_fusion.4
  2517.3 16.1 bitcast_reduce_fusion.4
  2545.9 16.1 bitcast_reduce_fusion.4
  2574.5 16.1 bitcast_reduce_fusion.4
  (185 shorter events, 276.7 us)
Async XLA Ops:
  7.2 32.5 %copy-start = (bf16[64,64]{1,0:T(8,128)(2,1)S(1)}, bf16[64,64]{1,0:T(8,128)(2,1)}, u32[]{:S(2)}) copy-start(bf16[64,64]{1,0:T(8,128)(2,1)} %param.22) | copy-start | bytes 24580
  7.2 943.5 %all-gather.13.cloned.1.call-start = ((), (), s32[]{:S(2)}) async-start(), calls=%async_computation.2 | async-start | bytes 41943040 | tf_op jit(solution)/shard_map/all_gather | solution.py:27
  7.2 6.7 copy-start.3
  7.2 11.1 copy-start.4
  18.3 8.2 copy-start.12
  18.3 8.2 copy-start.5
  39.7 8.5 copy-start.2
  39.7 8.5 copy-start.10
  59.8 1.0 copy-start.6
  59.8 1817.3 %all-gather.9.cloned.1.call-start = ((), (), s32[]{:S(2)}) async-start(), calls=%async_computation | async-start | bytes 41943040 | tf_op jit(solution)/shard_map/all_gather | solution.py:27
  85.6 0.7 copy-start.7
  85.6 12.2 copy-start.11
  85.6 1998.5 %all-gather.15.cloned.1.call-start = ((), (), s32[]{:S(2)}) async-start(), calls=%async_computation.3 | async-start | bytes 41943040 | tf_op jit(solution)/shard_map/all_gather | solution.py:29
  109.1 367.8 %collective-permute-start.1 = (bf16[256,256,64]{1,2,0:T(8,128)(2,1)S(1)}, bf16[256,256,64]{1,2,0:T(8,128)(2,1)}, u32[]{:S(2)}, u32[]{:S(2)}) collective-permute-start(bf16[256,256,64]{1,2,0:T(8,128)(2,1)S(1)} %multiply_convert_fusion.2), channel_id=1, source_target_pairs={{0,0},{4,1},{8,2},{12,3},{1,4},{5,5},{9,6},{13,7},{2,8},{6,9},{10,... | collective-permute-start | bytes 25165832 | tf_op jit(solution)/shard_map/ppermute | solution.py:28
  476.9 1862.8 %all-gather.11.cloned.1.call-start = ((), (), s32[]{:S(2)}) async-start(), calls=%async_computation.1 | async-start | bytes 41943040 | tf_op jit(solution)/shard_map/all_gather | solution.py:29
  499.8 278.0 %copy-start.8 = (bf16[64,64]{1,0:T(8,128)(2,1)S(1)}, bf16[64,64]{1,0:T(8,128)(2,1)}, u32[]{:S(2)}) copy-start(bf16[64,64]{1,0:T(8,128)(2,1)} %param.25) | copy-start | bytes 24580
  499.8 278.1 %copy-start.9 = (bf16[64,64]{1,0:T(8,128)(2,1)S(1)}, bf16[64,64]{1,0:T(8,128)(2,1)}, u32[]{:S(2)}) copy-start(bf16[64,64]{1,0:T(8,128)(2,1)} %param.26) | copy-start | bytes 24580
  499.8 277.9 %collective-permute-start = (bf16[256,256,64]{1,2,0:T(8,128)(2,1)S(1)}, bf16[256,256,64]{1,2,0:T(8,128)(2,1)}, u32[]{:S(2)}, u32[]{:S(2)}) collective-permute-start(bf16[256,256,64]{1,2,0:T(8,128)(2,1)S(1)} %multiply_convert_fusion.4), channel_id=1, source_target_pairs={{0,0},{4,1},{8,2},{12,3},{1,4},{5,5},{9,6},{13,7},{2,8},{6,9},{10,... | collective-permute-start | bytes 25165832 | tf_op jit(solution)/shard_map/ppermute | solution.py:28
  2107.5 4.5 copy-start.13
  2596.3 0.7 copy-start.1
Sparse Core Ops, SparseCore 0:
  59.9 890.6 all-gather.12
  952.2 924.8 all-gather.8
  1878.7 205.4 all-gather.14
  2085.6 202.1 all-gather.10
where the time goes:
time: 2620 us; the launch traced here: 2600 us
  waiting for transfers between devices  1840 us (70%)
  matrix products  430 us (16%)
  local copies, waits for them, and re-layouts  274 us (10%)
  other arithmetic  41.8 us (2%)
    all_gather x2, waiting for transfers between devices, tile_update(): left_rows = lax.all_gather(left, 'col', axis=1)  1040 us
    ppermute x2, waiting for transfers between devices, tile_update(): right_moved = lax.ppermute(right, ('col', 'row'), transpose_perm)  640 us
    dot_general x16, matrix products, finish(): jnp.einsum('itkc,tujkc->iujc', left_blk, right_rows, preferred_element_ty...  258 us
    all_gather x2, waiting for transfers between devices, tile_update(): lax.all_gather(right_moved, 'row', axis=0)  152 us
    dot_general x24, matrix products, project(): jnp.einsum('ijd,de->ije', source, weight, preferred_element_type=jnp.floa...  117 us
    reshape x2, local copies, waits for them, and re-layouts, tile_update(): left_rows.reshape(block_count, block_rows, col_count, cols_loc, hidden)  109 us
    dynamic_slice x16, local copies, waits for them, and re-layouts, tile_update(): lax.map(finish, (left_rows.reshape(block_count, block_rows, col_count, co...  107 us
    dot_general x16, matrix products, finish(): jnp.einsum('ijc,cd->ijd', normed_out, w_out, preferred_element_type=jnp.f...  55.2 us
  transfers between devices with their start and end apart: 6, of which 5 were waited for; matrix products, arithmetic and copies ran while one was open for 17% of the time, Pallas kernels for 0%

commit v1 on v0

v1 whole, which is shorter than its diff:
```python
import functools

import jax
import jax.numpy as jnp
from jax import lax
from jax.experimental import pallas as pl
from jax.experimental.pallas import tpu as pltpu
from jax.sharding import PartitionSpec as P

MESH = pl.DeviceIdType.MESH
F32 = jnp.float32
BF16 = jnp.bfloat16
G8 = 8


def norm_kernel(z0, z1, m0, m1, s, out):
    scale = s[...]
    for crop, (z, m) in enumerate(((z0, m0), (z1, m1))):
        v = z[...].astype(F32)
        v = v - jnp.mean(v, axis=1, keepdims=True)
        var = jnp.mean(v * v, axis=1, keepdims=True)
        x = (v * lax.rsqrt(var + 1e-5) * scale).astype(BF16)
        mask = m[...].astype(F32)[:, None, :]
        out[crop, 0] = (x.astype(F32) * mask).astype(BF16)


def finish_kernel(z, on, s, wg, wo, out):
    scale = s[...]
    for g in range(z.shape[0] // G8):
        rows = slice(g * G8, (g + 1) * G8)
        zf = z[rows].astype(F32)
        v = zf - jnp.mean(zf, axis=1, keepdims=True)
        var = jnp.mean(v * v, axis=1, keepdims=True)
        x = (v * lax.rsqrt(var + 1e-5) * scale).astype(BF16)
        k = x.shape[1] * G8
        gate = jnp.dot(wg[...], x.reshape(k, x.shape[2]), preferred_element_type=F32)
        half = jnp.dot(wo[...], on[0, g], preferred_element_type=F32)
        upd = ((1.0 + jnp.tanh(gate)) * half).reshape(zf.shape)
        out[rows] = (zf + upd).astype(BF16)


def tri_kernel(nch, ch, gx_in, wa, wb, so, on, gx, rx, A, B, O, xa, xb, st,
               g_sem, r_sem, s_in, s_out, s_f, s_r1, s_r2, l_sem, o_sem):
    del gx_in
    z = lax.axis_index("col")
    r = lax.axis_index("row")
    h = z // 2
    zz = z + h * (3 - 2 * z)
    q = r + h * (3 - 2 * r)
    inner = z + 1 - 2 * h
    outer = 3 * h
    partner = r + 1 - 2 * (r % 2)
    cross = 2 - h
    mid = zz == 1
    end = zz == 0
    owner = q == zz
    relay = q == 2
    n_i, n_k = gx.shape[2], gx.shape[4]
    cr = n_i // nch

    def rows(j):
        return pl.ds(pl.multiple_of(j * cr, cr), cr)

    def gs(c, t, j):
        return gx.at[c, t, rows(j)]

    def rs(c, t, j):
        return rx.at[c, t, rows(j)]

    def cp(src, dst, ssem, rsem, col, row):
        return pltpu.make_async_remote_copy(src_ref=src, dst_ref=dst, send_sem=ssem, recv_sem=rsem,
                                            device_id={"col": col, "row": row}, device_id_type=MESH)

    def p_in(c, j):
        return cp(gs(c, 0, j), gs(c, 1 + zz, j), s_in.at[c, j], g_sem.at[c, zz, j], inner, r)

    def p_out(c, j):
        return cp(gs(c, 0, j), gs(c, 1, j), s_out.at[c, j], g_sem.at[c, 0, j], outer, r)

    def fwd(n, c, j):
        src, dst, col = ((1, 3, inner), (2, 2, outer), (3, 3, outer))[n]
        return cp(gs(c, src, j), gs(c, dst, j), s_f.at[c, n, j], g_sem.at[c, dst - 1, j], col, r)

    def wait_g(c, t, j):
        cp(gs(c, t, j), gs(c, t, j), s_in.at[c, j], g_sem.at[c, t - 1, j], z, r).wait_recv()

    def rx_p(c, t, j):
        return cp(gs(c, t, j), rs(c, t, j), s_r1.at[c, t, j], r_sem.at[c, t, j], z, partner)

    def rx_c(c, t, j):
        return cp(gs(c, t, j), rs(c, t, j), s_r2.at[c, t, j], r_sem.at[c, t, j], z, cross)

    def rx_f(c, t, j):
        return cp(rs(c, t, j), rs(c, t, j), s_r1.at[c, t, j], r_sem.at[c, t, j], z, partner)

    def rx_send(c, t, j):
        rx_c(c, t, j).start()
        rx_p(c, t, j).start()

    @pl.loop(0, nch)
    def _(j):
        p_in(0, j).start()

        @pl.when(mid)
        def _():
            p_out(0, j).start()

        @pl.when(end)
        def _():
            p_in(1, j).start()

    def comm(c, t, j):
        @pl.when((c == 0) & (t == 0) & owner)
        def _():
            rx_send(0, 0, j)

        @pl.when((c == 0) & (t == 2) & owner)
        def _():
            rx_send(1, 0, j)

        @pl.when((c == 0) & (t == 2) & mid)
        def _():
            p_in(1, j).start()

        @pl.when((t == 1) & mid)
        def _():
            wait_g(c, 1, j)
            fwd(0, c, j).start()
            wait_g(c, 2, j)
            fwd(1, c, j).start()

            @pl.when(owner)
            def _():
                rx_send(c, 1, j)
                rx_send(c, 2, j)

        @pl.when((t == 3) & mid)
        def _():
            wait_g(c, 3, j)
            fwd(2, c, j).start()

            @pl.when(owner)
            def _():
                rx_send(c, 3, j)

            @pl.when(c == 0)
            def _():
                p_out(1, j).start()

        @pl.when((t > 0) & end)
        def _():
            for tt in (1, 2, 3):
                @pl.when(t == tt)
                def _():
                    wait_g(c, tt, j)

            @pl.when(owner)
            def _():
                rx_send(c, t, j)

    half = wa.shape[1] // 2

    def project(src, w, dst, j):
        @pl.loop(0, cr // 16)
        def _(s):
            xs = src[pl.ds(pl.multiple_of(s * 16, 16), 16)]
            x0 = xs[:G8].reshape(G8 * ch, n_k)
            x1 = xs[G8:].reshape(G8 * ch, n_k)
            i0 = pl.multiple_of(j * cr + s * 16, 16)
            nc = half // G8
            for p in range(w.shape[0]):
                parts = []
                for xg in (x0, x1):
                    res = jnp.dot(w[p], xg, preferred_element_type=F32)
                    val = res[:half] * (1.0 + jnp.tanh(res[half:]))
                    parts.append(val.reshape(nc, G8, n_k))
                dst[p * nc:(p + 1) * nc, pl.ds(i0, 16), :] = jnp.concatenate(parts, axis=1).astype(BF16)

    @pl.loop(0, 2)
    def _(c):
        @pl.loop(0, ch)
        def _(k):
            O[k] = jnp.zeros(O.shape[1:], F32)

        @pl.loop(0, 4)
        def _(t):
            @pl.loop(0, nch)
            def _(j):
                comm(c, t, j)
                la = pltpu.make_async_copy(gs(c, t, j), xa, l_sem.at[0])
                la.start()

                @pl.when(owner)
                def _():
                    pltpu.make_async_copy(gs(c, t, j), xb, l_sem.at[1]).start()

                la.wait()
                project(xa, wa, A, j)

                @pl.when(jnp.logical_not(owner))
                def _():
                    rx_p(c, t, j).wait_recv()

                    @pl.when(relay)
                    def _():
                        rx_f(c, t, j).start()

                    pltpu.make_async_copy(rs(c, t, j), xb, l_sem.at[1]).start()

                pltpu.make_async_copy(rs(c, t, j), xb, l_sem.at[1]).wait()
                project(xb, wb, B, j)

            @pl.loop(0, ch)
            def _(k):
                O[k] += lax.dot_general(A[k], B[k], (((1,), (1,)), ((), ())), preferred_element_type=F32)

        n_g = n_i // G8
        per = st.shape[1]

        def put(c, b):
            return pltpu.make_async_copy(st.at[b % 2], on.at[c, pl.ds(b * per, per)], o_sem.at[b % 2])

        @pl.loop(0, n_g // per)
        def _(b):
            @pl.when(b >= 2)
            def _():
                put(c, b - 2).wait()

            @pl.loop(0, per)
            def _(g):
                i0 = pl.multiple_of((b * per + g) * G8, G8)
                v = O[:, pl.ds(i0, G8), :]
                v = v - jnp.mean(v, axis=0, keepdims=True)
                var = jnp.mean(v * v, axis=0, keepdims=True)
                v = v * lax.rsqrt(var + 1e-5) * so[...]
                st[b % 2, g] = v.reshape(ch * G8, v.shape[2]).astype(BF16)

            put(c, b).start()

        put(c, n_g // per - 2).wait()
        put(c, n_g // per - 1).wait()

    @pl.loop(0, 2)
    def _(c):
        @pl.loop(0, nch)
        def _(j):
            p_in(c, j).wait_send()

            @pl.when(mid)
            def _():
                p_out(c, j).wait_send()
                for n in range(3):
                    fwd(n, c, j).wait_send()

            @pl.when(owner)
            def _():
                for t in range(4):
                    rx_c(c, t, j).wait_send()
                    rx_p(c, t, j).wait_send()

            @pl.when(relay)
            def _():
                for t in range(4):
                    rx_f(c, t, j).wait_send()


def spread(mat):
    eye = jnp.eye(G8, dtype=mat.dtype)
    n_o, n_c = mat.shape
    return (mat[:, None, None, :] * eye[None, :, :, None]).reshape(n_o * G8, G8 * n_c)


def solution(mesh):
    nch = 4

    def device_fn(z_one, z_two, mask_one, mask_two, ln_in_scale, w_a, w_a_gate, w_b, w_b_gate, w_gate, w_out, ln_out_scale):
        n_i, n_k, ch = z_one.shape
        zt = [jnp.swapaxes(v, 1, 2) for v in (z_one, z_two)]
        s_in = jnp.broadcast_to(ln_in_scale.astype(F32)[None, :, None], (1, ch, n_k))
        s_out = jnp.broadcast_to(ln_out_scale.astype(F32)[:, None, None], (ch, G8, n_k))

        def pair(w, wg):
            both = jnp.stack([w.T, wg.T]) * jnp.asarray(0.5, BF16)
            both = both.reshape(2, 2, ch // 2, ch).transpose(1, 0, 2, 3).reshape(2 * ch, ch)
            return spread(both).reshape(2, ch * G8, ch * G8)

        wa, wb = pair(w_a, w_a_gate), pair(w_b, w_b_gate)
        eye = jnp.eye(G8, dtype=BF16)
        wgt = w_gate.T * jnp.asarray(0.5, BF16)
        wot = w_out.T * jnp.asarray(0.5, BF16)
        wgk = (eye[:, None, :, None] * wgt[None, :, None, :]).reshape(G8 * ch, G8 * ch)
        wok = (eye[:, None, None, :] * wot[None, :, :, None]).reshape(G8 * ch, ch * G8)

        br = 16
        zspec = pl.BlockSpec((br, ch, n_k), lambda i: (i, 0, 0))
        mspec = pl.BlockSpec((br, n_k), lambda i: (i, 0))
        sspec = pl.BlockSpec((1, ch, n_k), lambda i: (0, 0, 0))
        xm = pl.pallas_call(
            norm_kernel,
            grid=(n_i // br,),
            in_specs=[zspec, zspec, mspec, mspec, sspec],
            out_specs=pl.BlockSpec((2, 1, br, ch, n_k), lambda i: (0, 0, i, 0, 0)),
            out_shape=jax.ShapeDtypeStruct((2, 4, n_i, ch, n_k), BF16),
            name="norm_in",
        )(zt[0], zt[1], mask_one, mask_two, s_in)

        n_g = n_i // G8
        anyspec = pl.BlockSpec(memory_space=pl.ANY)
        vspec = pl.BlockSpec(memory_space=pltpu.VMEM)
        dma = pltpu.SemaphoreType.DMA
        cr = n_i // nch
        on, _, _ = pl.pallas_call(
            functools.partial(tri_kernel, nch, ch),
            out_shape=(
                jax.ShapeDtypeStruct((2, n_g, ch * G8, n_k), BF16),
                jax.ShapeDtypeStruct((2, 4, n_i, ch, n_k), BF16),
                jax.ShapeDtypeStruct((2, 4, n_i, ch, n_k), BF16),
            ),
            in_specs=[anyspec, vspec, vspec, vspec],
            out_specs=(anyspec, anyspec, anyspec),
            input_output_aliases={0: 1},
            scratch_shapes=[
                pltpu.VMEM((ch, n_i, n_k), BF16),
                pltpu.VMEM((ch, n_k, n_k), BF16),
                pltpu.VMEM((ch, n_i, n_k), F32),
                pltpu.VMEM((cr, ch, n_k), BF16),
                pltpu.VMEM((cr, ch, n_k), BF16),
                pltpu.VMEM((2, 4, ch * G8, n_k), BF16),
                dma((2, 3, nch)),
                dma((2, 4, nch)),
                dma((2, nch)),
                dma((2, nch)),
                dma((2, 3, nch)),
                dma((2, 4, nch)),
                dma((2, 4, nch)),
                dma((2,)),
                dma((2,)),
            ],
            compiler_params=pltpu.CompilerParams(has_side_effects=True, vmem_limit_bytes=60 * 1024 * 1024),
            name="triangle",
        )(xm, wa, wb, s_out)

        outs = []
        for crop in range(2):
            out = pl.pallas_call(
                finish_kernel,
                grid=(n_i // br,),
                in_specs=[
                    zspec,
                    pl.BlockSpec((1, br // G8, ch * G8, n_k), lambda i, crop=crop: (crop, i, 0, 0)),
                    sspec,
                    pl.BlockSpec((G8 * ch, G8 * ch), lambda i: (0, 0)),
                    pl.BlockSpec((G8 * ch, ch * G8), lambda i: (0, 0)),
                ],
                out_specs=zspec,
                out_shape=jax.ShapeDtypeStruct((n_i, ch, n_k), BF16),
                name="finish",
            )(zt[crop], on, s_in, wgk, wok)
            outs.append(jnp.swapaxes(out, 1, 2))
        return tuple(outs)

    pair_spec = P(("batch", "row"), "col", None)
    mask_spec = P(("batch", "row"), "col")
    rep = P()
    return jax.shard_map(
        device_fn,
        mesh=mesh,
        in_specs=(pair_spec, pair_spec, mask_spec, mask_spec) + (rep,) * 8,
        out_specs=(pair_spec, pair_spec),
        check_vma=False,
    )
```

time: 2620 us -> 1250 us (0.48)
  waiting for transfers between devices: 1840 us -> 0 us
  Pallas kernels: 0 us -> 1240 us
  matrix products: 430 us -> 0 us
  local copies, waits for them, and re-layouts: 274 us -> 12 us
  other arithmetic: 41.8 us -> 2 us
    pallas_call x0 -> x4, Pallas kernels: none -> 1240 us  [the longest x1 1170 us: device_fn(): pl.pallas_call(functools.partial(tri_kernel, nch, ch), out_shape=(jax.Sha...]
    all_gather x4 -> x0, waiting for transfers between devices: 1200 us -> none  [the longest x2 1040 us: tile_update(): left_rows = lax.all_gather(left, 'col', axis=1)]
    ppermute x2 -> x0, waiting for transfers between devices: 640 us -> none  [tile_update(): right_moved = lax.ppermute(right, ('col', 'row'), transpose_perm)]
    dot_general x56 -> x0, matrix products: 430 us -> none  [the longest x16 258 us: finish(): jnp.einsum('itkc,tujkc->iujc', left_blk, right_rows, preferred_element_ty...]
    reshape x2 -> x0, local copies, waits for them, and re-layouts: 109 us -> none  [tile_update(): left_rows.reshape(block_count, block_rows, col_count, cols_loc, hidden)]
    dynamic_slice x16 -> x0, local copies, waits for them, and re-layouts: 107 us -> none  [tile_update(): lax.map(finish, (left_rows.reshape(block_count, block_rows, col_count, co...]
    while x4 -> x0, local copies, waits for them, and re-layouts: 46.8 us -> none  [tile_update(): lax.map(finish, (left_rows.reshape(block_count, block_rows, col_count, co...]
  transfers between devices with their start and end apart: 6 -> 0, of which waited for: 5 -> 0; matrix products, arithmetic and copies ran while one was open for 17% -> 0% of each run, Pallas kernels for 0% -> 0%
where the time goes in v1:
time: 1250 us
  Pallas kernels  1240 us (99%)
    pallas_call x1, Pallas kernels, device_fn(): pl.pallas_call(functools.partial(tri_kernel, nch, ch), out_shape=(jax.Sha...  1170 us
    pallas_call x2, Pallas kernels, device_fn(): pl.pallas_call(finish_kernel, grid=(n_i // br,), in_specs=[zspec, pl.Bloc...  39.9 us

profile of v1, /device:TPU:24, one launch (start us, length us, event | category | flops | bytes accessed | tf_op | source)
XLA Modules:
  0.0 1250.8 jit_solution(1229340637108507930)
XLA Ops:
  0.6 1.4 broadcast_in_dim.4.s
  2.0 0.0 copy-start
  2.0 0.0 copy-start.1
  2.0 0.0 copy-start.2
  2.0 0.0 copy-start.3
  2.0 22.5 %norm_in.1.gx_in = bf16[2,4,256,64,256]{4,3,2,1,0:T(8,128)(2,1)} custom-call(bf16[256,64,256]{2,1,0:T(8,128)(2,1)} %bitcast.38, bf16[256,64,256]{2,1,0:T(8,128)(2,1)} %bitcast.36, s32[256,256]{1,0:T(8,128)} %m0.1, s32[256,256]{1,0:T(8,128)} %m1.1, f32[1,64,256]{2,1,0:T(8,128)} %broadcast_in_dim.4.s), custom_call_target="tpu_custom_call" | custom-call | tf_op jit(solution)/shard_map/norm_in/pallas_call | solution.py:298
  24.5 0.0 copy-start.6
  24.5 0.1 copy.20
  24.6 0.0 copy-done
  24.6 0.1 copy.22
  24.7 0.0 copy-done.1
  24.7 0.1 copy.21
  24.8 0.0 copy-done.2
  24.8 0.1 copy.17
  24.9 0.0 copy-done.3
  24.9 0.1 copy.18
  25.1 1.7 broadcast_multiply_fusion
  26.7 4.0 mul.102.wb
  30.8 2.0 mul.97.wa
  32.8 0.0 copy-done.6
  32.8 0.9 broadcast_in_dim.5.so
  33.7 1173.7 %triangle.1 = (bf16[2,32,512,256]{3,2,1,0:T(8,128)(2,1)}, bf16[2,4,256,64,256]{4,3,2,1,0:T(8,128)(2,1)}, bf16[2,4,256,64,256]{4,3,2,1,0:T(8,128)(2,1)}) custom-call(bf16[2,4,256,64,256]{4,3,2,1,0:T(8,128)(2,1)} %norm_in.1.gx_in, bf16[2,512,512]{2,1,0:T(8,128)(2,1)} %mul.97.wa, bf16[2,512,512]{2,1,0:T(8,128)(2,1)} %mul.102.wb, ...), custom_call_target="tpu_custom_call", output_to_operand_aliasing={{1}: (0, {})} | custom-call | tf_op jit(solution)/shard_map/triangle/pallas_call | solution.py:312
  1207.4 0.0 copy-done.4
  1207.4 0.1 copy.25
  1207.5 0.1 broadcast_multiply_fusion.3
  1207.7 1.4 mul.108.wg
  1209.1 0.0 copy-done.5
  1209.1 0.1 broadcast_multiply_fusion.2
  1209.3 0.6 mul.114
  1209.9 1.0 copy.26.wo
  1210.9 19.9 %finish.3 = bf16[256,64,256]{2,1,0:T(8,128)(2,1)} custom-call(bf16[256,64,256]{2,1,0:T(8,128)(2,1)} %bitcast.37, bf16[2,32,512,256]{3,2,1,0:T(8,128)(2,1)} %get-tuple-element.3.on, f32[1,64,256]{2,1,0:T(8,128)} %broadcast_in_dim.4.s, bf16[512,512]{1,0:T(8,128)(2,1)} %mul.108.wg, bf16[512,512]{1,0:T(8,128)(2,1)} %copy.26.wo), custom_call_target="tpu_custom_call" | custom-call | tf_op jit(solution)/shard_map/finish/pallas_call | solution.py:345
  1230.8 20.0 %finish.2 = bf16[256,64,256]{2,1,0:T(8,128)(2,1)} custom-call(bf16[256,64,256]{2,1,0:T(8,128)(2,1)} %bitcast.39, bf16[2,32,512,256]{3,2,1,0:T(8,128)(2,1)} %get-tuple-element.3.on, f32[1,64,256]{2,1,0:T(8,128)} %broadcast_in_dim.4.s, bf16[512,512]{1,0:T(8,128)(2,1)} %mul.108.wg, bf16[512,512]{1,0:T(8,128)(2,1)} %copy.26.wo), custom_call_target="tpu_custom_call" | custom-call | tf_op jit(solution)/shard_map/finish/pallas_call | solution.py:345
  (9 shorter events, 0.1 us)
Async XLA Ops:
  2.0 22.6 %copy-start = (bf16[64,64]{1,0:T(8,128)(2,1)S(1)}, bf16[64,64]{1,0:T(8,128)(2,1)}, u32[]{:S(2)}) copy-start(bf16[64,64]{1,0:T(8,128)(2,1)} %param.20) | copy-start | bytes 24580
  2.0 22.7 %copy-start.1 = (bf16[64,64]{1,0:T(8,128)(2,1)S(1)}, bf16[64,64]{1,0:T(8,128)(2,1)}, u32[]{:S(2)}) copy-start(bf16[64,64]{1,0:T(8,128)(2,1)} %param.19) | copy-start | bytes 24580
  2.0 22.8 %copy-start.2 = (bf16[64,64]{1,0:T(8,128)(2,1)S(1)}, bf16[64,64]{1,0:T(8,128)(2,1)}, u32[]{:S(2)}) copy-start(bf16[64,64]{1,0:T(8,128)(2,1)} %param.17) | copy-start | bytes 24580
  2.0 22.9 %copy-start.3 = (bf16[64,64]{1,0:T(8,128)(2,1)S(1)}, bf16[64,64]{1,0:T(8,128)(2,1)}, u32[]{:S(2)}) copy-start(bf16[64,64]{1,0:T(8,128)(2,1)} %param.18) | copy-start | bytes 24580
  24.5 8.3 copy-start.6
  33.7 1173.7 %copy-start.4 = (bf16[64,64]{1,0:T(8,128)(2,1)S(1)}, bf16[64,64]{1,0:T(8,128)(2,1)}, u32[]{:S(2)}) copy-start(bf16[64,64]{1,0:T(8,128)(2,1)} %param.21) | copy-start | bytes 24580
  33.7 1175.4 %copy-start.5 = (bf16[64,64]{1,0:T(8,128)(2,1)S(1)}, bf16[64,64]{1,0:T(8,128)(2,1)}, u32[]{:S(2)}) copy-start(bf16[64,64]{1,0:T(8,128)(2,1)} %param.22) | copy-start | bytes 24580

commit v2 on v1

--- a/solution.py
+++ b/solution.py
@@ -39,8 +39,8 @@
         out[rows] = (zf + upd).astype(BF16)
 
 
-def tri_kernel(nch, ch, gx_in, wa, wb, so, on, gx, rx, A, B, O, xa, xb, st,
-               g_sem, r_sem, s_in, s_out, s_f, s_r1, s_r2, l_sem, o_sem):
+def tri_kernel(nch, ch, gx_in, wa, wb, so, on, gx, rx, r2, ex, A, B, O, xa, xb, st,
+               g_sem, r_sem, r2_sem, t_sem, s_in, s_out, s_f, s_r1, s_r2, s_x, s_t, l_sem, o_sem):
     del gx_in
     z = lax.axis_index("col")
     r = lax.axis_index("row")
@@ -53,10 +53,21 @@
     cross = 2 - h
     mid = zz == 1
     end = zz == 0
+    even = q % 2 == 0
     owner = q == zz
-    relay = q == 2
+    wide_owner = mid & (q == 1)
+    relay = mid & (q == 2)
+    rx_here = (mid & (q != 1)) | (end & (q == 2))
+    extra = mid & (q < 2)
+    has_own = mid | even
+    r2_from = mid & ((q == 0) | (q == 3))
+    r2_row = (1 - (q // 3)) * partner + (q // 3) * 3 * h
+    t_row = (1 - q) * (3 - 3 * h) + q * r
     n_i, n_k = gx.shape[2], gx.shape[4]
     cr = n_i // nch
+    n_g = n_i // G8
+    per = st.shape[1]
+    n_b = n_g // per
 
     def rows(j):
         return pl.ds(pl.multiple_of(j * cr, cr), cr)
@@ -66,6 +77,9 @@
 
     def rs(c, t, j):
         return rx.at[c, t, rows(j)]
+
+    def r2s(c, t, j):
+        return r2.at[c, t, rows(j)]
 
     def cp(src, dst, ssem, rsem, col, row):
         return pltpu.make_async_remote_copy(src_ref=src, dst_ref=dst, send_sem=ssem, recv_sem=rsem,
@@ -93,15 +107,33 @@
     def rx_f(c, t, j):
         return cp(rs(c, t, j), rs(c, t, j), s_r1.at[c, t, j], r_sem.at[c, t, j], z, partner)
 
-    def rx_send(c, t, j):
-        rx_c(c, t, j).start()
-        rx_p(c, t, j).start()
+    def r2_c(c, t, j):
+        return cp(gs(c, t, j), r2s(c, t, j), s_x.at[c, t, j], r2_sem.at[c, t, j], z, r2_row)
+
+    def tile(ref, c, b):
+        return ref.at[c, pl.ds(pl.multiple_of(b * per, per), per)]
+
+    def t_c(c, b):
+        return cp(tile(ex, c, b), tile(on, c, b), s_t.at[c, b], t_sem.at[c, b], outer, t_row)
+
+    def side_sends(c, t, j):
+        @pl.when(owner)
+        def _():
+            rx_c(c, t, j).start()
+
+        @pl.when(wide_owner)
+        def _():
+            rx_p(c, t, j).start()
+
+        @pl.when(r2_from)
+        def _():
+            r2_c(c, t, j).start()
 
     @pl.loop(0, nch)
     def _(j):
         p_in(0, j).start()
 
-        @pl.when(mid)
+        @pl.when(mid & even)
         def _():
             p_out(0, j).start()
 
@@ -110,42 +142,43 @@
             p_in(1, j).start()
 
     def comm(c, t, j):
-        @pl.when((c == 0) & (t == 0) & owner)
-        def _():
-            rx_send(0, 0, j)
-
-        @pl.when((c == 0) & (t == 2) & owner)
-        def _():
-            rx_send(1, 0, j)
-
-        @pl.when((c == 0) & (t == 2) & mid)
-        def _():
-            p_in(1, j).start()
+        @pl.when((c == 0) & (t == 0))
+        def _():
+            side_sends(0, 0, j)
+
+        @pl.when((c == 0) & (t == 2))
+        def _():
+            side_sends(1, 0, j)
+
+            @pl.when(mid)
+            def _():
+                p_in(1, j).start()
 
         @pl.when((t == 1) & mid)
         def _():
             wait_g(c, 1, j)
             fwd(0, c, j).start()
+            side_sends(c, 1, j)
             wait_g(c, 2, j)
-            fwd(1, c, j).start()
-
-            @pl.when(owner)
-            def _():
-                rx_send(c, 1, j)
-                rx_send(c, 2, j)
+
+            @pl.when(even)
+            def _():
+                fwd(1, c, j).start()
+
+            side_sends(c, 2, j)
 
         @pl.when((t == 3) & mid)
         def _():
             wait_g(c, 3, j)
-            fwd(2, c, j).start()
-
-            @pl.when(owner)
-            def _():
-                rx_send(c, 3, j)
-
-            @pl.when(c == 0)
-            def _():
-                p_out(1, j).start()
+            side_sends(c, 3, j)
+
+            @pl.when(even)
+            def _():
+                fwd(2, c, j).start()
+
+                @pl.when(c == 0)
+                def _():
+                    p_out(1, j).start()
 
         @pl.when((t > 0) & end)
         def _():
@@ -153,10 +186,7 @@
                 @pl.when(t == tt)
                 def _():
                     wait_g(c, tt, j)
-
-            @pl.when(owner)
-            def _():
-                rx_send(c, t, j)
+                    side_sends(c, tt, j)
 
     half = wa.shape[1] // 2
 
@@ -176,92 +206,168 @@
                     parts.append(val.reshape(nc, G8, n_k))
                 dst[p * nc:(p + 1) * nc, pl.ds(i0, 16), :] = jnp.concatenate(parts, axis=1).astype(BF16)
 
-    @pl.loop(0, 2)
-    def _(c):
+    def load(ref, c, t, j, dst, n):
+        return pltpu.make_async_copy(ref.at[c, t, rows(j)], dst, l_sem.at[n])
+
+    def steps(c, t, p):
+        a_r2 = (p == 0) & (q == 0)
+        b_r2 = (p == 0) & (q == 1)
+        b_rx = (p == 1) & rx_here
+        a_new = (p == 0) | jnp.logical_not(extra & (q == 1))
+
+        @pl.loop(0, nch)
+        def _(j):
+            @pl.when((p == 0) | jnp.logical_not(extra))
+            def _():
+                comm(c, t, j)
+
+            @pl.when(jnp.logical_not(b_rx | b_r2))
+            def _():
+                load(gx, c, t, j, xb, 1).start()
+
+            @pl.when(a_new)
+            def _():
+                @pl.when(a_r2)
+                def _():
+                    r2_c(c, t, j).wait_recv()
+                    load(r2, c, t, j, xa, 0).start()
+
+                @pl.when(jnp.logical_not(a_r2))
+                def _():
+                    load(gx, c, t, j, xa, 0).start()
+
+                load(gx, c, t, j, xa, 0).wait()
+                project(xa, wa, A, j)
+
+            @pl.when(b_r2)
+            def _():
+                r2_c(c, t, j).wait_recv()
+                load(r2, c, t, j, xb, 1).start()
+
+            @pl.when(b_rx)
+            def _():
+                rx_p(c, t, j).wait_recv()
+
+                @pl.when(relay)
+                def _():
+                    rx_f(c, t, j).start()
+
+                load(rx, c, t, j, xb, 1).start()
+
+            load(gx, c, t, j, xb, 1).wait()
+            project(xb, wb, B, j)
+
         @pl.loop(0, ch)
         def _(k):
-            O[k] = jnp.zeros(O.shape[1:], F32)
-
-        @pl.loop(0, 4)
-        def _(t):
-            @pl.loop(0, nch)
-            def _(j):
-                comm(c, t, j)
-                la = pltpu.make_async_copy(gs(c, t, j), xa, l_sem.at[0])
-                la.start()
-
-                @pl.when(owner)
-                def _():
-                    pltpu.make_async_copy(gs(c, t, j), xb, l_sem.at[1]).start()
-
-                la.wait()
-                project(xa, wa, A, j)
-
-                @pl.when(jnp.logical_not(owner))
-                def _():
-                    rx_p(c, t, j).wait_recv()
-
-                    @pl.when(relay)
-                    def _():
-                        rx_f(c, t, j).start()
-
-                    pltpu.make_async_copy(rs(c, t, j), xb, l_sem.at[1]).start()
-
-                pltpu.make_async_copy(rs(c, t, j), xb, l_sem.at[1]).wait()
-                project(xb, wb, B, j)
-
-            @pl.loop(0, ch)
-            def _(k):
-                O[k] += lax.dot_general(A[k], B[k], (((1,), (1,)), ((), ())), preferred_element_type=F32)
-
-        n_g = n_i // G8
-        per = st.shape[1]
-
-        def put(c, b):
-            return pltpu.make_async_copy(st.at[b % 2], on.at[c, pl.ds(b * per, per)], o_sem.at[b % 2])
-
-        @pl.loop(0, n_g // per)
+            prod = lax.dot_general(A[k], B[k], (((1,), (1,)), ((), ())), preferred_element_type=F32)
+
+            @pl.when(t == 0)
+            def _():
+                O[p, k] = prod
+
+            @pl.when(t > 0)
+            def _():
+                O[p, k] += prod
+
+    def put(c, b, p):
+        src = st.at[b % 2]
+
+        @pl.when(p == 0)
+        def _():
+            pltpu.make_async_copy(src, tile(ex, c, b), o_sem.at[b % 2]).start()
+
+        @pl.when(p == 1)
+        def _():
+            pltpu.make_async_copy(src, tile(on, c, b), o_sem.at[b % 2]).start()
+
+    def put_done(c, b, p):
+        pltpu.make_async_copy(st.at[b % 2], tile(ex, c, b), o_sem.at[b % 2]).wait()
+
+        @pl.when(p == 0)
+        def _():
+            t_c(c, b).start()
+
+    def close(c, p):
+        @pl.loop(0, n_b)
         def _(b):
-            @pl.when(b >= 2)
-            def _():
-                put(c, b - 2).wait()
-
             @pl.loop(0, per)
             def _(g):
                 i0 = pl.multiple_of((b * per + g) * G8, G8)
-                v = O[:, pl.ds(i0, G8), :]
+                v = O[p, :, pl.ds(i0, G8), :]
                 v = v - jnp.mean(v, axis=0, keepdims=True)
                 var = jnp.mean(v * v, axis=0, keepdims=True)
                 v = v * lax.rsqrt(var + 1e-5) * so[...]
                 st[b % 2, g] = v.reshape(ch * G8, v.shape[2]).astype(BF16)
 
-            put(c, b).start()
-
-        put(c, n_g // per - 2).wait()
-        put(c, n_g // per - 1).wait()
+            put(c, b, p)
+
+            @pl.when(b >= 1)
+            def _():
+                put_done(c, b - 1, p)
+
+        put_done(c, n_b - 1, p)
+
+    @pl.when(has_own)
+    def _():
+        @pl.loop(0, 2)
+        def _(c):
+            @pl.loop(0, 4)
+            def _(t):
+                @pl.loop(0, 2)
+                def _(p):
+                    @pl.when((p == 1) | extra)
+                    def _():
+                        steps(c, t, p)
+
+                        @pl.when(t == 3)
+                        def _():
+                            close(c, p)
 
     @pl.loop(0, 2)
     def _(c):
+        @pl.when(end & jnp.logical_not(even))
+        def _():
+            @pl.loop(0, n_b)
+            def _(b):
+                t_c(c, b).wait_recv()
+
+        @pl.when(extra)
+        def _():
+            @pl.loop(0, n_b)
+            def _(b):
+                t_c(c, b).wait_send()
+
         @pl.loop(0, nch)
         def _(j):
             p_in(c, j).wait_send()
 
             @pl.when(mid)
             def _():
-                p_out(c, j).wait_send()
-                for n in range(3):
-                    fwd(n, c, j).wait_send()
-
-            @pl.when(owner)
-            def _():
-                for t in range(4):
+                fwd(0, c, j).wait_send()
+
+                @pl.when(even)
+                def _():
+                    p_out(c, j).wait_send()
+                    fwd(1, c, j).wait_send()
+                    fwd(2, c, j).wait_send()
+
+            @pl.loop(0, 4)
+            def _(t):
+                @pl.when(owner)
+                def _():
                     rx_c(c, t, j).wait_send()
+
+                @pl.when(wide_owner)
+                def _():
                     rx_p(c, t, j).wait_send()
 
-            @pl.when(relay)
-            def _():
-                for t in range(4):
+                @pl.when(relay)
+                def _():
                     rx_f(c, t, j).wait_send()
+
+                @pl.when(r2_from)
+                def _():
+                    r2_c(c, t, j).wait_send()
 
 
 def spread(mat):
@@ -309,30 +415,37 @@
         vspec = pl.BlockSpec(memory_space=pltpu.VMEM)
         dma = pltpu.SemaphoreType.DMA
         cr = n_i // nch
-        on, _, _ = pl.pallas_call(
+        per = 4
+        on, _, _, _, _ = pl.pallas_call(
             functools.partial(tri_kernel, nch, ch),
             out_shape=(
                 jax.ShapeDtypeStruct((2, n_g, ch * G8, n_k), BF16),
                 jax.ShapeDtypeStruct((2, 4, n_i, ch, n_k), BF16),
                 jax.ShapeDtypeStruct((2, 4, n_i, ch, n_k), BF16),
+                jax.ShapeDtypeStruct((2, 4, n_i, ch, n_k), BF16),
+                jax.ShapeDtypeStruct((2, n_g, ch * G8, n_k), BF16),
             ),
             in_specs=[anyspec, vspec, vspec, vspec],
-            out_specs=(anyspec, anyspec, anyspec),
+            out_specs=(anyspec,) * 5,
             input_output_aliases={0: 1},
             scratch_shapes=[
                 pltpu.VMEM((ch, n_i, n_k), BF16),
                 pltpu.VMEM((ch, n_k, n_k), BF16),
-                pltpu.VMEM((ch, n_i, n_k), F32),
+                pltpu.VMEM((2, ch, n_i, n_k), F32),
                 pltpu.VMEM((cr, ch, n_k), BF16),
                 pltpu.VMEM((cr, ch, n_k), BF16),
-                pltpu.VMEM((2, 4, ch * G8, n_k), BF16),
+                pltpu.VMEM((2, per, ch * G8, n_k), BF16),
                 dma((2, 3, nch)),
                 dma((2, 4, nch)),
+                dma((2, 4, nch)),
+                dma((2, n_g // per)),
                 dma((2, nch)),
                 dma((2, nch)),
                 dma((2, 3, nch)),
                 dma((2, 4, nch)),
                 dma((2, 4, nch)),
+                dma((2, 4, nch)),
+                dma((2, n_g // per)),
                 dma((2,)),
                 dma((2,)),
             ],

time: 1250 us -> 1450 us (1.16)
  Pallas kernels: 1240 us -> 1440 us
    pallas_call x1, Pallas kernels: 1170 us -> 1370 us  [device_fn(): pl.pallas_call(functools.partial(tri_kernel, nch, ch), out_shape=(jax.Sha...]
where the time goes in v2:
time: 1450 us
  Pallas kernels  1440 us (99%)
    pallas_call x1, Pallas kernels, device_fn(): pl.pallas_call(functools.partial(tri_kernel, nch, ch), out_shape=(jax.Sha...  1370 us
    pallas_call x2, Pallas kernels, device_fn(): pl.pallas_call(finish_kernel, grid=(n_i // br,), in_specs=[zspec, pl.Bloc...  39.9 us

profile of v2, /device:TPU:24, one launch (start us, length us, event | category | flops | bytes accessed | tf_op | source)
XLA Modules:
  0.0 1450.0 jit_solution(9867672535058042982)
XLA Ops:
  0.6 1.3 broadcast_in_dim.4.s
  2.0 0.0 copy-start
  2.0 0.0 copy-start.1
  2.0 0.0 copy-start.2
  2.0 0.0 copy-start.3
  2.0 22.5 %norm_in.1.gx_in = bf16[2,4,256,64,256]{4,3,2,1,0:T(8,128)(2,1)} custom-call(bf16[256,64,256]{2,1,0:T(8,128)(2,1)} %bitcast.38, bf16[256,64,256]{2,1,0:T(8,128)(2,1)} %bitcast.36, s32[256,256]{1,0:T(8,128)} %m0.1, s32[256,256]{1,0:T(8,128)} %m1.1, f32[1,64,256]{2,1,0:T(8,128)} %broadcast_in_dim.4.s), custom_call_target="tpu_custom_call" | custom-call | tf_op jit(solution)/shard_map/norm_in/pallas_call | solution.py:404
  24.5 0.0 copy-start.6
  24.5 0.1 copy.20
  24.6 0.0 copy-done
  24.6 0.1 copy.22
  24.7 0.0 copy-done.1
  24.7 0.1 copy.21
  24.8 0.0 copy-done.2
  24.8 0.1 copy.17
  24.9 0.0 copy-done.3
  24.9 0.1 copy.18
  25.0 1.7 broadcast_multiply_fusion
  26.7 4.0 mul.102.wb
  30.8 2.0 mul.97.wa
  32.8 0.0 copy-done.6
  32.8 1.0 broadcast_in_dim.5.so
  33.7 1372.8 %triangle.1 = (bf16[2,32,512,256]{3,2,1,0:T(8,128)(2,1)}, bf16[2,4,256,64,256]{4,3,2,1,0:T(8,128)(2,1)}, bf16[2,4,256,64,256]{4,3,2,1,0:T(8,128)(2,1)}, bf16[2,4...) custom-call(bf16[2,4,256,64,256]{4,3,2,1,0:T(8,128)(2,1)} %norm_in.1.gx_in, ...), custom_call_target="tpu_custom_call", output_to_operand_aliasing={{1}: (0, {})} | custom-call | tf_op jit(solution)/shard_map/triangle/pallas_call | solution.py:419
  1406.6 0.0 copy-done.4
  1406.6 0.1 copy.25
  1406.7 0.1 broadcast_multiply_fusion.3
  1406.9 1.4 mul.108.wg
  1408.3 0.0 copy-done.5
  1408.3 0.1 broadcast_multiply_fusion.2
  1408.4 0.6 mul.114
  1409.1 1.0 copy.26.wo
  1410.1 19.9 %finish.3 = bf16[256,64,256]{2,1,0:T(8,128)(2,1)} custom-call(bf16[256,64,256]{2,1,0:T(8,128)(2,1)} %bitcast.37, bf16[2,32,512,256]{3,2,1,0:T(8,128)(2,1)} %get-tuple-element.3.on, f32[1,64,256]{2,1,0:T(8,128)} %broadcast_in_dim.4.s, bf16[512,512]{1,0:T(8,128)(2,1)} %mul.108.wg, bf16[512,512]{1,0:T(8,128)(2,1)} %copy.26.wo), custom_call_target="tpu_custom_call" | custom-call | tf_op jit(solution)/shard_map/finish/pallas_call | solution.py:458
  1430.0 20.0 %finish.2 = bf16[256,64,256]{2,1,0:T(8,128)(2,1)} custom-call(bf16[256,64,256]{2,1,0:T(8,128)(2,1)} %bitcast.39, bf16[2,32,512,256]{3,2,1,0:T(8,128)(2,1)} %get-tuple-element.3.on, f32[1,64,256]{2,1,0:T(8,128)} %broadcast_in_dim.4.s, bf16[512,512]{1,0:T(8,128)(2,1)} %mul.108.wg, bf16[512,512]{1,0:T(8,128)(2,1)} %copy.26.wo), custom_call_target="tpu_custom_call" | custom-call | tf_op jit(solution)/shard_map/finish/pallas_call | solution.py:458
  (9 shorter events, 0.1 us)
Async XLA Ops:
  2.0 22.6 %copy-start = (bf16[64,64]{1,0:T(8,128)(2,1)S(1)}, bf16[64,64]{1,0:T(8,128)(2,1)}, u32[]{:S(2)}) copy-start(bf16[64,64]{1,0:T(8,128)(2,1)} %param.20) | copy-start | bytes 24580
  2.0 22.7 %copy-start.1 = (bf16[64,64]{1,0:T(8,128)(2,1)S(1)}, bf16[64,64]{1,0:T(8,128)(2,1)}, u32[]{:S(2)}) copy-start(bf16[64,64]{1,0:T(8,128)(2,1)} %param.19) | copy-start | bytes 24580
  2.0 22.8 %copy-start.2 = (bf16[64,64]{1,0:T(8,128)(2,1)S(1)}, bf16[64,64]{1,0:T(8,128)(2,1)}, u32[]{:S(2)}) copy-start(bf16[64,64]{1,0:T(8,128)(2,1)} %param.17) | copy-start | bytes 24580
  2.0 22.9 %copy-start.3 = (bf16[64,64]{1,0:T(8,128)(2,1)S(1)}, bf16[64,64]{1,0:T(8,128)(2,1)}, u32[]{:S(2)}) copy-start(bf16[64,64]{1,0:T(8,128)(2,1)} %param.18) | copy-start | bytes 24580
  24.5 8.3 copy-start.6
  33.7 1372.9 %copy-start.4 = (bf16[64,64]{1,0:T(8,128)(2,1)S(1)}, bf16[64,64]{1,0:T(8,128)(2,1)}, u32[]{:S(2)}) copy-start(bf16[64,64]{1,0:T(8,128)(2,1)} %param.21) | copy-start | bytes 24580
  33.7 1374.5 %copy-start.5 = (bf16[64,64]{1,0:T(8,128)(2,1)S(1)}, bf16[64,64]{1,0:T(8,128)(2,1)}, u32[]{:S(2)}) copy-start(bf16[64,64]{1,0:T(8,128)(2,1)} %param.22) | copy-start | bytes 24580

commit v3 on v2

--- a/solution.py
+++ b/solution.py
@@ -132,6 +132,7 @@
     @pl.loop(0, nch)
     def _(j):
         p_in(0, j).start()
+        side_sends(0, 0, j)
 
         @pl.when(mid & even)
         def _():
@@ -141,52 +142,56 @@
         def _():
             p_in(1, j).start()
 
+    def comm_near(c, j):
+        wait_g(c, 1, j)
+
+        @pl.when(mid)
+        def _():
+            fwd(0, c, j).start()
+
+        side_sends(c, 1, j)
+        wait_g(c, 2, j)
+
+        @pl.when(mid & even)
+        def _():
+            fwd(1, c, j).start()
+
+        side_sends(c, 2, j)
+
+    def comm_far(c, j):
+        @pl.when((c == 0) & mid)
+        def _():
+            p_in(1, j).start()
+
+        wait_g(c, 3, j)
+
+        @pl.when(mid & even)
+        def _():
+            fwd(2, c, j).start()
+
+        side_sends(c, 3, j)
+
+        @pl.when(c == 0)
+        def _():
+            side_sends(1, 0, j)
+
+            @pl.when(mid & even)
+            def _():
+                p_out(1, j).start()
+
     def comm(c, t, j):
-        @pl.when((c == 0) & (t == 0))
-        def _():
-            side_sends(0, 0, j)
-
-        @pl.when((c == 0) & (t == 2))
-        def _():
-            side_sends(1, 0, j)
-
-            @pl.when(mid)
-            def _():
-                p_in(1, j).start()
-
-        @pl.when((t == 1) & mid)
-        def _():
-            wait_g(c, 1, j)
-            fwd(0, c, j).start()
-            side_sends(c, 1, j)
-            wait_g(c, 2, j)
-
-            @pl.when(even)
-            def _():
-                fwd(1, c, j).start()
-
-            side_sends(c, 2, j)
-
-        @pl.when((t == 3) & mid)
-        def _():
-            wait_g(c, 3, j)
-            side_sends(c, 3, j)
-
-            @pl.when(even)
-            def _():
-                fwd(2, c, j).start()
-
-                @pl.when(c == 0)
-                def _():
-                    p_out(1, j).start()
-
-        @pl.when((t > 0) & end)
-        def _():
-            for tt in (1, 2, 3):
-                @pl.when(t == tt)
-                def _():
-                    wait_g(c, tt, j)
-                    side_sends(c, tt, j)
+        u = t * nch + j
+        v = u % 8
+        jj = v - 3 + (6 - v) // 4
+        hit = (v == 2) | ((v >= 4) & (v <= 6))
+
+        @pl.when(hit & (u < 8))
+        def _():
+            comm_near(c, jj)
+
+        @pl.when(hit & (u >= 8))
+        def _():
+            comm_far(c, jj)
 
     half = wa.shape[1] // 2
 

time: 1450 us -> 1310 us (0.903)
  Pallas kernels: 1440 us -> 1290 us
    pallas_call x1, Pallas kernels: 1370 us -> 1230 us  [device_fn(): pl.pallas_call(functools.partial(tri_kernel, nch, ch), out_shape=(jax.Sha...]
where the time goes in v3:
time: 1310 us
  Pallas kernels  1290 us (98%)
    pallas_call x1, Pallas kernels, device_fn(): pl.pallas_call(functools.partial(tri_kernel, nch, ch), out_shape=(jax.Sha...  1230 us
    pallas_call x2, Pallas kernels, device_fn(): pl.pallas_call(finish_kernel, grid=(n_i // br,), in_specs=[zspec, pl.Bloc...  39.9 us

profile of v3, /device:TPU:24, one launch (start us, length us, event | category | flops | bytes accessed | tf_op | source)
XLA Modules:
  0.0 1306.3 jit_solution(12600910831995133254)
XLA Ops:
  0.6 1.3 broadcast_in_dim.4.s
  2.0 0.0 copy-start
  2.0 0.0 copy-start.1
  2.0 0.0 copy-start.2
  2.0 0.0 copy-start.3
  2.0 22.5 %norm_in.1.gx_in = bf16[2,4,256,64,256]{4,3,2,1,0:T(8,128)(2,1)} custom-call(bf16[256,64,256]{2,1,0:T(8,128)(2,1)} %bitcast.38, bf16[256,64,256]{2,1,0:T(8,128)(2,1)} %bitcast.36, s32[256,256]{1,0:T(8,128)} %m0.1, s32[256,256]{1,0:T(8,128)} %m1.1, f32[1,64,256]{2,1,0:T(8,128)} %broadcast_in_dim.4.s), custom_call_target="tpu_custom_call" | custom-call | tf_op jit(solution)/shard_map/norm_in/pallas_call | solution.py:409
  24.5 0.0 copy-start.6
  24.5 0.1 copy.20
  24.6 0.0 copy-done
  24.6 0.1 copy.22
  24.7 0.0 copy-done.1
  24.7 0.1 copy.21
  24.8 0.0 copy-done.2
  24.8 0.1 copy.17
  24.9 0.0 copy-done.3
  24.9 0.1 copy.18
  25.0 1.7 broadcast_multiply_fusion
  26.7 4.0 mul.102.wb
  30.8 2.0 mul.97.wa
  32.8 0.0 copy-done.6
  32.8 1.0 broadcast_in_dim.5.so
  33.7 1229.2 %triangle.1 = (bf16[2,32,512,256]{3,2,1,0:T(8,128)(2,1)}, bf16[2,4,256,64,256]{4,3,2,1,0:T(8,128)(2,1)}, bf16[2,4,256,64,256]{4,3,2,1,0:T(8,128)(2,1)}, bf16[2,4...) custom-call(bf16[2,4,256,64,256]{4,3,2,1,0:T(8,128)(2,1)} %norm_in.1.gx_in, ...), custom_call_target="tpu_custom_call", output_to_operand_aliasing={{1}: (0, {})} | custom-call | tf_op jit(solution)/shard_map/triangle/pallas_call | solution.py:424
  1262.9 0.0 copy-done.4
  1263.0 0.1 copy.25
  1263.1 0.1 broadcast_multiply_fusion.3
  1263.2 1.4 mul.108.wg
  1264.6 0.0 copy-done.5
  1264.6 0.1 broadcast_multiply_fusion.2
  1264.8 0.6 mul.114
  1265.4 1.0 copy.26.wo
  1266.4 19.9 %finish.3 = bf16[256,64,256]{2,1,0:T(8,128)(2,1)} custom-call(bf16[256,64,256]{2,1,0:T(8,128)(2,1)} %bitcast.37, bf16[2,32,512,256]{3,2,1,0:T(8,128)(2,1)} %get-tuple-element.3.on, f32[1,64,256]{2,1,0:T(8,128)} %broadcast_in_dim.4.s, bf16[512,512]{1,0:T(8,128)(2,1)} %mul.108.wg, bf16[512,512]{1,0:T(8,128)(2,1)} %copy.26.wo), custom_call_target="tpu_custom_call" | custom-call | tf_op jit(solution)/shard_map/finish/pallas_call | solution.py:463
  1286.4 20.0 %finish.2 = bf16[256,64,256]{2,1,0:T(8,128)(2,1)} custom-call(bf16[256,64,256]{2,1,0:T(8,128)(2,1)} %bitcast.39, bf16[2,32,512,256]{3,2,1,0:T(8,128)(2,1)} %get-tuple-element.3.on, f32[1,64,256]{2,1,0:T(8,128)} %broadcast_in_dim.4.s, bf16[512,512]{1,0:T(8,128)(2,1)} %mul.108.wg, bf16[512,512]{1,0:T(8,128)(2,1)} %copy.26.wo), custom_call_target="tpu_custom_call" | custom-call | tf_op jit(solution)/shard_map/finish/pallas_call | solution.py:463
  (9 shorter events, 0.1 us)
Async XLA Ops:
  2.0 22.6 %copy-start = (bf16[64,64]{1,0:T(8,128)(2,1)S(1)}, bf16[64,64]{1,0:T(8,128)(2,1)}, u32[]{:S(2)}) copy-start(bf16[64,64]{1,0:T(8,128)(2,1)} %param.20) | copy-start | bytes 24580
  2.0 22.7 %copy-start.1 = (bf16[64,64]{1,0:T(8,128)(2,1)S(1)}, bf16[64,64]{1,0:T(8,128)(2,1)}, u32[]{:S(2)}) copy-start(bf16[64,64]{1,0:T(8,128)(2,1)} %param.19) | copy-start | bytes 24580
  2.0 22.8 %copy-start.2 = (bf16[64,64]{1,0:T(8,128)(2,1)S(1)}, bf16[64,64]{1,0:T(8,128)(2,1)}, u32[]{:S(2)}) copy-start(bf16[64,64]{1,0:T(8,128)(2,1)} %param.17) | copy-start | bytes 24580
  2.0 22.9 %copy-start.3 = (bf16[64,64]{1,0:T(8,128)(2,1)S(1)}, bf16[64,64]{1,0:T(8,128)(2,1)}, u32[]{:S(2)}) copy-start(bf16[64,64]{1,0:T(8,128)(2,1)} %param.18) | copy-start | bytes 24580
  24.5 8.3 copy-start.6
  33.7 1229.2 %copy-start.4 = (bf16[64,64]{1,0:T(8,128)(2,1)S(1)}, bf16[64,64]{1,0:T(8,128)(2,1)}, u32[]{:S(2)}) copy-start(bf16[64,64]{1,0:T(8,128)(2,1)} %param.21) | copy-start | bytes 24580
  33.7 1230.9 %copy-start.5 = (bf16[64,64]{1,0:T(8,128)(2,1)S(1)}, bf16[64,64]{1,0:T(8,128)(2,1)}, u32[]{:S(2)}) copy-start(bf16[64,64]{1,0:T(8,128)(2,1)} %param.22) | copy-start | bytes 24580

commit v4 on v3

--- a/solution.py
+++ b/solution.py
@@ -13,33 +13,69 @@
 G8 = 8
 
 
-def norm_kernel(z0, z1, m0, m1, s, out):
+def grow(w, first, count, rows_inner, cols_inner):
+    k, m = w.shape
+    i_r, i_m = (lax.broadcasted_iota(jnp.int32, (G8 * count, m), d) for d in (0, 1))
+    i_k, i_c = (lax.broadcasted_iota(jnp.int32, (k, G8 * k), d) for d in (0, 1))
+    pick_r = ((i_r // G8 if rows_inner else i_r % count) + first == i_m).astype(F32).astype(BF16)
+    pick_c = ((i_c // G8 if cols_inner else i_c % k) == i_k).astype(F32).astype(BF16)
+    big = lax.dot_general(pick_r, w, (((1,), (1,)), ((), ())), preferred_element_type=F32).astype(BF16)
+    big = jnp.dot(big, pick_c, preferred_element_type=F32) * 0.5
+    b_r, b_c = (lax.broadcasted_iota(jnp.int32, (G8 * count, G8 * k), d) for d in (0, 1))
+    row_r = b_r % G8 if rows_inner else b_r // count
+    row_c = b_c % G8 if cols_inner else b_c // k
+    return jnp.where(row_r == row_c, big, 0.0).astype(BF16)
+
+
+def layer_norm_row(zf, scale, keep):
+    v = zf - jnp.mean(zf, axis=0, keepdims=True)
+    rstd = lax.rsqrt(jnp.mean(v * v, axis=0, keepdims=True) + 1e-5)
+    if keep is not None:
+        rstd = rstd * keep
+    return v * rstd * scale
+
+
+def norm_kernel(z0, z1, m0, m1, s, wa, wag, wb, wbg, wg, wo, out, w_ab, w_g, w_o):
+    @pl.when(pl.program_id(0) == 0)
+    def _():
+        ch = wa.shape[0]
+        hc = ch // 2
+        for side, ws in enumerate(((wa, wag), (wb, wbg))):
+            for p in range(2):
+                for kind in range(2):
+                    part = slice(kind * hc * G8, (kind + 1) * hc * G8)
+                    w_ab[side, p, part, :] = grow(ws[kind][...], p * hc, hc, True, False)
+        w_g[...] = grow(wg[...], 0, ch, False, False)
+        w_o[...] = grow(wo[...], 0, ch, False, True)
+
     scale = s[...]
     for crop, (z, m) in enumerate(((z0, m0), (z1, m1))):
-        v = z[...].astype(F32)
-        v = v - jnp.mean(v, axis=1, keepdims=True)
-        var = jnp.mean(v * v, axis=1, keepdims=True)
-        x = (v * lax.rsqrt(var + 1e-5) * scale).astype(BF16)
-        mask = m[...].astype(F32)[:, None, :]
-        out[crop, 0] = (x.astype(F32) * mask).astype(BF16)
-
-
-def finish_kernel(z, on, s, wg, wo, out):
+        @pl.loop(0, z.shape[0] // G8)
+        def _(g):
+            i0 = pl.multiple_of(g * G8, G8)
+            keep = m[pl.ds(i0, G8), :].astype(F32)
+            for d in range(G8):
+                x = layer_norm_row(z[i0 + d].astype(F32), scale, keep[d:d + 1])
+                out[crop, 0, i0 + d] = x.astype(BF16)
+
+
+def finish_kernel(z0, z1, on0, on1, s, wg, wo, out0, out1):
     scale = s[...]
-    for g in range(z.shape[0] // G8):
-        rows = slice(g * G8, (g + 1) * G8)
-        zf = z[rows].astype(F32)
-        v = zf - jnp.mean(zf, axis=1, keepdims=True)
-        var = jnp.mean(v * v, axis=1, keepdims=True)
-        x = (v * lax.rsqrt(var + 1e-5) * scale).astype(BF16)
-        k = x.shape[1] * G8
-        gate = jnp.dot(wg[...], x.reshape(k, x.shape[2]), preferred_element_type=F32)
-        half = jnp.dot(wo[...], on[0, g], preferred_element_type=F32)
-        upd = ((1.0 + jnp.tanh(gate)) * half).reshape(zf.shape)
-        out[rows] = (zf + upd).astype(BF16)
-
-
-def tri_kernel(nch, ch, gx_in, wa, wb, so, on, gx, rx, r2, ex, A, B, O, xa, xb, st,
+    for z, on, out in ((z0, on0, out0), (z1, on1, out1)):
+        ch, n_k = z.shape[1:]
+        for g in range(z.shape[0] // G8):
+            half = jnp.dot(wo[...], on[0, g], preferred_element_type=F32)
+            for d in range(0, G8, 4):
+                r = g * G8 + d
+                x = jnp.concatenate(
+                    [layer_norm_row(z[r + e].astype(F32), scale, None).astype(BF16) for e in range(4)], axis=0)
+                gate = jnp.dot(wg[:4 * ch, :4 * ch], x, preferred_element_type=F32)
+                upd = (1.0 + jnp.tanh(gate)) * half[d * ch:(d + 4) * ch]
+                for e in range(4):
+                    out[r + e] = (z[r + e].astype(F32) + upd[e * ch:(e + 1) * ch]).astype(BF16)
+
+
+def tri_kernel(nch, ch, gx_in, w, so, on, gx, rx, r2, ex, AB, O, xb, st,
                g_sem, r_sem, r2_sem, t_sem, s_in, s_out, s_f, s_r1, s_r2, s_x, s_t, l_sem, o_sem):
     del gx_in
     z = lax.axis_index("col")
@@ -193,32 +229,36 @@
         def _():
             comm_far(c, jj)
 
-    half = wa.shape[1] // 2
-
-    def project(src, w, dst, j):
+    half = w.shape[2] // 2
+
+    def project(buf, sel, j):
         @pl.loop(0, cr // 16)
         def _(s):
-            xs = src[pl.ds(pl.multiple_of(s * 16, 16), 16)]
+            xs = xb[buf, pl.ds(pl.multiple_of(s * 16, 16), 16)]
             x0 = xs[:G8].reshape(G8 * ch, n_k)
             x1 = xs[G8:].reshape(G8 * ch, n_k)
             i0 = pl.multiple_of(j * cr + s * 16, 16)
             nc = half // G8
-            for p in range(w.shape[0]):
+            for p in range(w.shape[1]):
                 parts = []
                 for xg in (x0, x1):
-                    res = jnp.dot(w[p], xg, preferred_element_type=F32)
+                    res = jnp.dot(w[sel, p], xg, preferred_element_type=F32)
                     val = res[:half] * (1.0 + jnp.tanh(res[half:]))
                     parts.append(val.reshape(nc, G8, n_k))
-                dst[p * nc:(p + 1) * nc, pl.ds(i0, 16), :] = jnp.concatenate(parts, axis=1).astype(BF16)
-
-    def load(ref, c, t, j, dst, n):
-        return pltpu.make_async_copy(ref.at[c, t, rows(j)], dst, l_sem.at[n])
+                AB[sel, p * nc:(p + 1) * nc, pl.ds(i0, 16), :] = jnp.concatenate(parts, axis=1).astype(BF16)
+
+    def load(ref, c, t, j, buf):
+        return pltpu.make_async_copy(ref.at[c, t, rows(j)], xb.at[buf], l_sem.at[buf])
 
     def steps(c, t, p):
-        a_r2 = (p == 0) & (q == 0)
-        b_r2 = (p == 0) & (q == 1)
-        b_rx = (p == 1) & rx_here
-        a_new = (p == 0) | jnp.logical_not(extra & (q == 1))
+        first_b = (p == 0) & (q == 0)
+        from_r2 = p == 0
+        from_rx = (p == 1) & rx_here
+        remote = from_r2 | from_rx
+        keep_a = (p == 1) & extra & (q == 1)
+        sel1 = first_b.astype(jnp.int32)
+        sel2 = 1 - sel1
+        again = ((p == 0) & extra).astype(jnp.int32)
 
         @pl.loop(0, nch)
         def _(j):
@@ -226,30 +266,12 @@
             def _():
                 comm(c, t, j)
 
-            @pl.when(jnp.logical_not(b_rx | b_r2))
-            def _():
-                load(gx, c, t, j, xb, 1).start()
-
-            @pl.when(a_new)
-            def _():
-                @pl.when(a_r2)
-                def _():
-                    r2_c(c, t, j).wait_recv()
-                    load(r2, c, t, j, xa, 0).start()
-
-                @pl.when(jnp.logical_not(a_r2))
-                def _():
-                    load(gx, c, t, j, xa, 0).start()
-
-                load(gx, c, t, j, xa, 0).wait()
-                project(xa, wa, A, j)
-
-            @pl.when(b_r2)
+            @pl.when(from_r2)
             def _():
                 r2_c(c, t, j).wait_recv()
-                load(r2, c, t, j, xb, 1).start()
-
-            @pl.when(b_rx)
+                load(r2, c, t, j, 2).start()
+
+            @pl.when(from_rx)
             def _():
                 rx_p(c, t, j).wait_recv()
 
@@ -257,22 +279,48 @@
                 def _():
                     rx_f(c, t, j).start()
 
-                load(rx, c, t, j, xb, 1).start()
-
-            load(gx, c, t, j, xb, 1).wait()
-            project(xb, wb, B, j)
-
-        @pl.loop(0, ch)
-        def _(k):
-            prod = lax.dot_general(A[k], B[k], (((1,), (1,)), ((), ())), preferred_element_type=F32)
-
-            @pl.when(t == 0)
-            def _():
-                O[p, k] = prod
-
-            @pl.when(t > 0)
-            def _():
-                O[p, k] += prod
+                load(rx, c, t, j, 2).start()
+
+            buf = j % 2
+            load(gx, c, t, j, buf).wait()
+            at = 4 * c + t
+            last = (j + 1) // nch
+            nxt = at + last * (1 - again)
+            nj = (j + 1) % nch
+
+            @pl.when(nxt < 8)
+            def _():
+                load(gx, nxt // 4, nxt % 4, nj, 1 - buf).start()
+
+            @pl.when(jnp.logical_not(keep_a))
+            def _():
+                project(buf, sel1, j)
+
+            @pl.when(remote)
+            def _():
+                load(rx, c, t, j, 2).wait()
+
+            rem = remote.astype(jnp.int32)
+            project(buf * (1 - rem) + 2 * rem, sel2, j)
+
+        step = 4
+
+        def product(k):
+            return lax.dot_general(AB[0, k], AB[1, k], (((1,), (1,)), ((), ())), preferred_element_type=F32)
+
+        @pl.when(t == 0)
+        def _():
+            @pl.loop(0, ch // step)
+            def _(k):
+                for d in range(step):
+                    O[p, k * step + d] = product(k * step + d)
+
+        @pl.when(t > 0)
+        def _():
+            @pl.loop(0, ch // step)
+            def _(k):
+                for d in range(step):
+                    O[p, k * step + d] += product(k * step + d)
 
     def put(c, b, p):
         src = st.at[b % 2]
@@ -314,6 +362,8 @@
 
     @pl.when(has_own)
     def _():
+        load(gx, 0, 0, 0, 0).start()
+
         @pl.loop(0, 2)
         def _(c):
             @pl.loop(0, 4)
@@ -375,52 +425,47 @@
                     r2_c(c, t, j).wait_send()
 
 
-def spread(mat):
-    eye = jnp.eye(G8, dtype=mat.dtype)
-    n_o, n_c = mat.shape
-    return (mat[:, None, None, :] * eye[None, :, :, None]).reshape(n_o * G8, G8 * n_c)
-
-
 def solution(mesh):
     nch = 4
 
     def device_fn(z_one, z_two, mask_one, mask_two, ln_in_scale, w_a, w_a_gate, w_b, w_b_gate, w_gate, w_out, ln_out_scale):
         n_i, n_k, ch = z_one.shape
         zt = [jnp.swapaxes(v, 1, 2) for v in (z_one, z_two)]
-        s_in = jnp.broadcast_to(ln_in_scale.astype(F32)[None, :, None], (1, ch, n_k))
+        s_in = jnp.broadcast_to(ln_in_scale.astype(F32)[:, None], (ch, n_k))
         s_out = jnp.broadcast_to(ln_out_scale.astype(F32)[:, None, None], (ch, G8, n_k))
-
-        def pair(w, wg):
-            both = jnp.stack([w.T, wg.T]) * jnp.asarray(0.5, BF16)
-            both = both.reshape(2, 2, ch // 2, ch).transpose(1, 0, 2, 3).reshape(2 * ch, ch)
-            return spread(both).reshape(2, ch * G8, ch * G8)
-
-        wa, wb = pair(w_a, w_a_gate), pair(w_b, w_b_gate)
-        eye = jnp.eye(G8, dtype=BF16)
-        wgt = w_gate.T * jnp.asarray(0.5, BF16)
-        wot = w_out.T * jnp.asarray(0.5, BF16)
-        wgk = (eye[:, None, :, None] * wgt[None, :, None, :]).reshape(G8 * ch, G8 * ch)
-        wok = (eye[:, None, None, :] * wot[None, :, :, None]).reshape(G8 * ch, ch * G8)
-
         br = 16
         zspec = pl.BlockSpec((br, ch, n_k), lambda i: (i, 0, 0))
         mspec = pl.BlockSpec((br, n_k), lambda i: (i, 0))
-        sspec = pl.BlockSpec((1, ch, n_k), lambda i: (0, 0, 0))
-        xm = pl.pallas_call(
+
+        def fixed(*shape):
+            return pl.BlockSpec(shape, lambda i: (0,) * len(shape))
+
+        big = G8 * ch
+        xm, w_ab, w_g, w_o = pl.pallas_call(
             norm_kernel,
             grid=(n_i // br,),
-            in_specs=[zspec, zspec, mspec, mspec, sspec],
-            out_specs=pl.BlockSpec((2, 1, br, ch, n_k), lambda i: (0, 0, i, 0, 0)),
-            out_shape=jax.ShapeDtypeStruct((2, 4, n_i, ch, n_k), BF16),
+            in_specs=[zspec, zspec, mspec, mspec, fixed(ch, n_k)] + [fixed(ch, ch)] * 6,
+            out_specs=(
+                pl.BlockSpec((2, 1, br, ch, n_k), lambda i: (0, 0, i, 0, 0)),
+                fixed(2, 2, big, big),
+                fixed(big, big),
+                fixed(big, big),
+            ),
+            out_shape=(
+                jax.ShapeDtypeStruct((2, 4, n_i, ch, n_k), BF16),
+                jax.ShapeDtypeStruct((2, 2, big, big), BF16),
+                jax.ShapeDtypeStruct((big, big), BF16),
+                jax.ShapeDtypeStruct((big, big), BF16),
+            ),
             name="norm_in",
-        )(zt[0], zt[1], mask_one, mask_two, s_in)
+        )(zt[0], zt[1], mask_one, mask_two, s_in, w_a, w_a_gate, w_b, w_b_gate, w_gate, w_out)
 
         n_g = n_i // G8
         anyspec = pl.BlockSpec(memory_space=pl.ANY)
         vspec = pl.BlockSpec(memory_space=pltpu.VMEM)
         dma = pltpu.SemaphoreType.DMA
         cr = n_i // nch
-        per = 4
+        per = 2
         on, _, _, _, _ = pl.pallas_call(
             functools.partial(tri_kernel, nch, ch),
             out_shape=(
@@ -430,15 +475,13 @@
                 jax.ShapeDtypeStruct((2, 4, n_i, ch, n_k), BF16),
                 jax.ShapeDtypeStruct((2, n_g, ch * G8, n_k), BF16),
             ),
-            in_specs=[anyspec, vspec, vspec, vspec],
+            in_specs=[anyspec, vspec, vspec],
             out_specs=(anyspec,) * 5,
             input_output_aliases={0: 1},
             scratch_shapes=[
-                pltpu.VMEM((ch, n_i, n_k), BF16),
-                pltpu.VMEM((ch, n_k, n_k), BF16),
+                pltpu.VMEM((2, ch, n_i, n_k), BF16),
                 pltpu.VMEM((2, ch, n_i, n_k), F32),
-                pltpu.VMEM((cr, ch, n_k), BF16),
-                pltpu.VMEM((cr, ch, n_k), BF16),
+                pltpu.VMEM((3, cr, ch, n_k), BF16),
                 pltpu.VMEM((2, per, ch * G8, n_k), BF16),
                 dma((2, 3, nch)),
                 dma((2, 4, nch)),
@@ -451,31 +494,23 @@
                 dma((2, 4, nch)),
                 dma((2, 4, nch)),
                 dma((2, n_g // per)),
-                dma((2,)),
+                dma((3,)),
                 dma((2,)),
             ],
-            compiler_params=pltpu.CompilerParams(has_side_effects=True, vmem_limit_bytes=60 * 1024 * 1024),
+            compiler_params=pltpu.CompilerParams(has_side_effects=True, vmem_limit_bytes=63 * 1024 * 1024),
             name="triangle",
-        )(xm, wa, wb, s_out)
-
-        outs = []
-        for crop in range(2):
-            out = pl.pallas_call(
-                finish_kernel,
-                grid=(n_i // br,),
-                in_specs=[
-                    zspec,
-                    pl.BlockSpec((1, br // G8, ch * G8, n_k), lambda i, crop=crop: (crop, i, 0, 0)),
-                    sspec,
-                    pl.BlockSpec((G8 * ch, G8 * ch), lambda i: (0, 0)),
-                    pl.BlockSpec((G8 * ch, ch * G8), lambda i: (0, 0)),
-                ],
-                out_specs=zspec,
-                out_shape=jax.ShapeDtypeStruct((n_i, ch, n_k), BF16),
-                name="finish",
-            )(zt[crop], on, s_in, wgk, wok)
-            outs.append(jnp.swapaxes(out, 1, 2))
-        return tuple(outs)
+        )(xm, w_ab, s_out)
+
+        onspec = [pl.BlockSpec((1, br // G8, big, n_k), lambda i, crop=crop: (crop, i, 0, 0)) for crop in range(2)]
+        outs = pl.pallas_call(
+            finish_kernel,
+            grid=(n_i // br,),
+            in_specs=[zspec, zspec, *onspec, fixed(ch, n_k), fixed(big, big), fixed(big, big)],
+            out_specs=(zspec, zspec),
+            out_shape=(jax.ShapeDtypeStruct((n_i, ch, n_k), BF16),) * 2,
+            name="finish",
+        )(zt[0], zt[1], on, on, s_in, w_g, w_o)
+        return tuple(jnp.swapaxes(out, 1, 2) for out in outs)
 
     pair_spec = P(("batch", "row"), "col", None)
     mask_spec = P(("batch", "row"), "col")

time: 1310 us -> 1230 us (0.939)
  the two profiles are of different devices: /device:TPU:24 before, /device:TPU:25 now
where the time goes in v4:
time: 1230 us
  Pallas kernels  1220 us (99%)
    pallas_call x1, Pallas kernels, device_fn(): pl.pallas_call(functools.partial(tri_kernel, nch, ch), out_shape=(jax.Sha...  1170 us
    pallas_call x1, Pallas kernels, device_fn(): pl.pallas_call(finish_kernel, grid=(n_i // br,), in_specs=[zspec, zspec,...  27.1 us
    pallas_call x1, Pallas kernels, device_fn(): pl.pallas_call(norm_kernel, grid=(n_i // br,), in_specs=[zspec, zspec, ms...  25 us

profile of v4, /device:TPU:25, one launch (start us, length us, event | category | flops | bytes accessed | tf_op | source)
XLA Modules:
  0.0 1225.6 jit_solution(9910990606459785324)
XLA Ops:
  0.6 1.4 broadcast_in_dim.4.s
  2.0 1.6 broadcast_in_dim.5.so
  3.6 25.0 %norm_in.1 = (bf16[2,4,256,64,256]{4,3,2,1,0:T(8,128)(2,1)}, bf16[2,2,512,512]{3,2,1,0:T(8,128)(2,1)}, bf16[512,512]{1,0:T(8,128)(2,1)}, bf16[512,512]{1,0:T(8,128)(2,1)}) custom-call(bf16[256,64,256]{2,1,0:T(8,128)(2,1)} %bitcast.4, bf16[256,64,256]{2,1,0:T(8,128)(2,1)} %bitcast.6, s32[256,256]{1,0:T(8,128)} %m0.1, s32[256,256]{1,0:T(8,128)} %m1.1, ...), custom_call_target="tpu_custom_call" | custom-call | tf_op jit(solution)/shard_map/norm_in/pallas_call | solution.py:444
  28.6 1169.9 %triangle.1 = (bf16[2,32,512,256]{3,2,1,0:T(8,128)(2,1)}, bf16[2,4,256,64,256]{4,3,2,1,0:T(8,128)(2,1)}, bf16[2,4,256,64,256]{4,3,2,1,0:T(8,128)(2,1)}, bf16[2,4...) custom-call(bf16[2,4,256,64,256]{4,3,2,1,0:T(8,128)(2,1)} %get-tuple-element.9.gx_in, ...), custom_call_target="tpu_custom_call", output_to_operand_aliasing={{1}: (0, {})} | custom-call | tf_op jit(solution)/shard_map/triangle/pallas_call | solution.py:469
  1198.5 27.1 %finish.1 = (bf16[256,64,256]{2,1,0:T(8,128)(2,1)}, bf16[256,64,256]{2,1,0:T(8,128)(2,1)}) custom-call(bf16[256,64,256]{2,1,0:T(8,128)(2,1)} %bitcast.5, bf16[256,64,256]{2,1,0:T(8,128)(2,1)} %bitcast.7, bf16[2,32,512,256]{3,2,1,0:T(8,128)(2,1)} %get-tuple-element.11.on0.on1, bf16[2,32,512,256]{3,2,1,0:T(8,128)(2,1)} %get-tuple-element.11.on0.on1, ...), custom_call_target="tpu_custom_call" | custom-call | tf_op jit(solution)/shard_map/finish/pallas_call | solution.py:505

commit v5 on v4

--- a/solution.py
+++ b/solution.py
@@ -174,8 +174,10 @@
         def _():
             p_out(0, j).start()
 
-        @pl.when(end)
-        def _():
+    @pl.when(end)
+    def _():
+        @pl.loop(0, nch)
+        def _(j):
             p_in(1, j).start()
 
     def comm_near(c, j):

time: 1230 us -> 1140 us (0.927)
  the two profiles are of different devices: /device:TPU:25 before, /device:TPU:4 now
where the time goes in v5:
time: 1140 us; the launch traced here: 1130 us
  Pallas kernels  1130 us (99%)
    pallas_call x1, Pallas kernels, device_fn(): pl.pallas_call(functools.partial(tri_kernel, nch, ch), out_shape=(jax.Sha...  1080 us
    pallas_call x1, Pallas kernels, device_fn(): pl.pallas_call(finish_kernel, grid=(n_i // br,), in_specs=[zspec, zspec,...  27.1 us
    pallas_call x1, Pallas kernels, device_fn(): pl.pallas_call(norm_kernel, grid=(n_i // br,), in_specs=[zspec, zspec, ms...  25 us

profile of v5, /device:TPU:4, one launch (start us, length us, event | category | flops | bytes accessed | tf_op | source)
XLA Modules:
  0.0 1134.5 jit_solution(13022500833355468878)
XLA Ops:
  0.6 1.4 broadcast_in_dim.4.s
  2.0 1.6 broadcast_in_dim.5.so
  3.6 25.0 %norm_in.1 = (bf16[2,4,256,64,256]{4,3,2,1,0:T(8,128)(2,1)}, bf16[2,2,512,512]{3,2,1,0:T(8,128)(2,1)}, bf16[512,512]{1,0:T(8,128)(2,1)}, bf16[512,512]{1,0:T(8,128)(2,1)}) custom-call(bf16[256,64,256]{2,1,0:T(8,128)(2,1)} %bitcast.4, bf16[256,64,256]{2,1,0:T(8,128)(2,1)} %bitcast.6, s32[256,256]{1,0:T(8,128)} %m0.1, s32[256,256]{1,0:T(8,128)} %m1.1, ...), custom_call_target="tpu_custom_call" | custom-call | tf_op jit(solution)/shard_map/norm_in/pallas_call | solution.py:446
  28.6 1078.8 %triangle.1 = (bf16[2,32,512,256]{3,2,1,0:T(8,128)(2,1)}, bf16[2,4,256,64,256]{4,3,2,1,0:T(8,128)(2,1)}, bf16[2,4,256,64,256]{4,3,2,1,0:T(8,128)(2,1)}, bf16[2,4...) custom-call(bf16[2,4,256,64,256]{4,3,2,1,0:T(8,128)(2,1)} %get-tuple-element.9.gx_in, ...), custom_call_target="tpu_custom_call", output_to_operand_aliasing={{1}: (0, {})} | custom-call | tf_op jit(solution)/shard_map/triangle/pallas_call | solution.py:471
  1107.4 27.1 %finish.1 = (bf16[256,64,256]{2,1,0:T(8,128)(2,1)}, bf16[256,64,256]{2,1,0:T(8,128)(2,1)}) custom-call(bf16[256,64,256]{2,1,0:T(8,128)(2,1)} %bitcast.5, bf16[256,64,256]{2,1,0:T(8,128)(2,1)} %bitcast.7, bf16[2,32,512,256]{3,2,1,0:T(8,128)(2,1)} %get-tuple-element.11.on0.on1, bf16[2,32,512,256]{3,2,1,0:T(8,128)(2,1)} %get-tuple-element.11.on0.on1, ...), custom_call_target="tpu_custom_call" | custom-call | tf_op jit(solution)/shard_map/finish/pallas_call | solution.py:507
